TPU v7x, 512 devices: a whole 4x8x8 slice. The times are simulated.
512 devices in a mesh: coil: 32 (over x, z), frame: 16 (over y, core).
Axes of the slice: x: 4, y: 8, z: 8, core: 2. Of those that a mesh axis runs over, the one named last changes fastest.
Arguments:
- initial_image: float32 [256, 16, 2, 256], P('coil', 'frame'), may hold values from -3 to 3
- coil_maps: bfloat16 [32, 2, 256, 256], P('coil'), may hold values from -1.5 to 1.5
- samples: bfloat16 [32, 16, 18, 2, 256], P('coil', 'frame'), may hold values from -6 to 6
- blocks_used: int32 [16], P('frame'), may hold values from 1 to 18, 145 in all
- row_offset: int32 [16, 18], P('frame'), may hold values from 0 to 128
- col_offset: int32 [16, 18], P('frame'), may hold values from 0 to 128
- row_first: int32 [16, 18, 256], P('frame'), may hold values from 0 to 124
- col_first: int32 [16, 18, 256], P('frame'), may hold values from 0 to 124
- row_taps: bfloat16 [16, 18, 4, 256], P('frame'), may hold values from 0.099609375 to 0.59765625
- col_taps: bfloat16 [16, 18, 4, 256], P('frame'), may hold values from 0.099609375 to 0.59765625
Outputs:
- image: float32 [256, 16, 2, 256], P('coil', 'frame')
- misfit: float32 [2, 16], P(None, 'frame')
Inputs may be any that keep to these rules, and one draw needn't show every extreme that they name: Blocks 0 to blocks_used minus one of the frame were acquired. `row_first`: the kernel's 4 rows lie inside the tile. `col_first`: the kernel's 4 columns lie inside the tile.
All inputs are finite; a program needn't handle non-finite values.
Results may differ from a plain program's by a relative error of at most 0.006.
Values may be sent and summed in bfloat16 or wider, within the bound.
A program may use at most 64 MiB of HBM per device.

v0:
```python
import functools
import math

import jax
import jax.numpy as jnp
import ml_dtypes
import numpy as np
from jax import lax
from jax.experimental import pallas as pl
from jax.experimental.pallas import tpu as pltpu
from jax.sharding import PartitionSpec as P

ITERS = 2
GROUP = 6
LANES = 128

step_size = 2.0
tv_weight = 0.1
smooth_floor = 0.5
shrink_weight = 0.1

F32 = jnp.float32
BF16 = jnp.bfloat16
MESH = pl.DeviceIdType.MESH


def table_pair(order):
    counter = np.arange(order)
    angle = (counter[:, None] * counter[None, :] % order) * (2.0 * math.pi / order)
    cosine = (np.cos(angle) / math.sqrt(order)).astype(ml_dtypes.bfloat16)
    sine = (np.sin(angle) / math.sqrt(order)).astype(ml_dtypes.bfloat16)
    return np.concatenate([cosine, sine], axis=1)


def partner_of(place, k, count):
    if count & (count - 1):
        return lax.rem(place + k, count)
    result, bit = 0, 1
    while bit < count:
        digit = place // bit % 2
        result = result + (1 - digit if k & bit else digit) * bit
        bit *= 2
    return result


def owner_of(place, k, count):
    if count & (count - 1):
        return lax.rem(place + count - k, count)
    return partner_of(place, k, count)


def dot(left, right):
    return jnp.dot(left, right, preferred_element_type=F32)


def dot_nt(left, right):
    return lax.dot_general(left, right, (((1,), (1,)), ((), ())), preferred_element_type=F32)


def partner(values, axis, parity):
    size = values.shape[axis]
    return jnp.where(
        parity == 0, pltpu.roll(values, size - 1, axis), pltpu.roll(values, 1, axis)
    )


def shrink_pair(real, imag, limit):
    length = jnp.sqrt(real * real + imag * imag)
    factor = jnp.maximum(length - limit, 0.0) / jnp.maximum(length, limit)
    return real * factor, imag * factor


def wavelet_prox(fields, limit):
    shape = fields[0].shape
    row_parity = lax.broadcasted_iota(jnp.int32, shape, 0) % 2
    col_parity = lax.broadcasted_iota(jnp.int32, shape, 1) % 2
    row_sign = jnp.where(row_parity == 0, 1.0, -1.0)
    col_sign = jnp.where(col_parity == 0, 1.0, -1.0)
    parts = []
    for field in fields:
        beside = partner(field, 1, col_parity)
        col_sum = field + beside
        col_diff = (field - beside) * col_sign
        sum_below = partner(col_sum, 0, row_parity)
        diff_below = partner(col_diff, 0, row_parity)
        approx = (col_sum + sum_below) * 0.5
        horiz = (col_diff + diff_below) * 0.5
        vertical = (col_sum - sum_below) * row_sign * 0.5
        diagonal = (col_diff - diff_below) * row_sign * 0.5
        parts.append((approx, horiz, vertical, diagonal))
    real, imag = parts
    horiz = shrink_pair(real[1], imag[1], limit)
    vertical = shrink_pair(real[2], imag[2], limit)
    diagonal = shrink_pair(real[3], imag[3], limit)
    return [
        (parts[p][0] + col_sign * horiz[p] + row_sign * vertical[p] + row_sign * col_sign * diagonal[p])
        for p in range(2)
    ]


def kernel(
    coils,
    frames,
    *refs,
):
    inputs = refs[:11]
    image_ref, misfit_ref = refs[11:13]
    held = refs[13:24]
    input_sem = refs[24]
    loads = []
    for place, (source, target) in enumerate(zip(inputs, held)):
        copy = pltpu.make_async_copy(source, target, input_sem.at[place])
        copy.start()
        loads.append(copy)
    run(coils, frames, loads, *held, image_ref, misfit_ref, *refs[25:])


def run(
    coils,
    frames,
    loads,
    start_ref,
    maps_ref,
    samples_ref,
    used_ref,
    row_off_ref,
    col_off_ref,
    row_first_ref,
    col_first_ref,
    row_taps_ref,
    col_taps_ref,
    table_ref,
    image_ref,
    misfit_ref,
    forward_ref,
    inverse_ref,
    row_ref,
    col_ref,
    stack_ref,
    space_ref,
    grid_ref,
    grad_ref,
    moving_ref,
    current_ref,
    low_ref,
    gather_ref,
    outgo_ref,
    income_ref,
    beside_ref,
    tally_ref,
    tallies_ref,
    gather_send,
    gather_recv,
    income_send,
    income_recv,
    beside_send,
    beside_recv,
    tally_send,
    tally_recv,
):
    coil = lax.axis_index("coil")
    frame = lax.axis_index("frame")
    size = maps_ref.shape[2]
    blocks = samples_ref.shape[2]
    spoke = samples_ref.shape[4]
    taps = row_taps_ref.shape[2]
    rows = size // coils
    later = lax.rem(frame + 1, frames)
    earlier = lax.rem(frame + frames - 1, frames)
    peers = [partner_of(coil, k, coils) for k in range(coils)]
    owners = [owner_of(coil, k, coils) for k in range(coils)]
    order = list(range(coils - 1, 0, -1))
    wire = gather_ref.dtype

    barrier = pltpu.get_barrier_semaphore()
    for k in range(1, coils):
        pl.semaphore_signal(barrier, inc=1, device_id={"coil": peers[k]}, device_id_type=MESH)
    for nearby in (later, earlier):
        pl.semaphore_signal(barrier, inc=1, device_id={"frame": nearby}, device_id_type=MESH)
    loads[0].wait()
    for p in range(2):
        value = start_ref[:, 0, p, :]
        low_ref[0, p] = value.astype(BF16).astype(wire)
        moving_ref[0, p] = value
        current_ref[p] = value
    pl.semaphore_wait(barrier, coils - 1 + 2)

    pending = []

    def send(source, target, send_sem, recv_sem, where):
        copy = pltpu.make_async_remote_copy(
            src_ref=source,
            dst_ref=target,
            send_sem=send_sem,
            recv_sem=recv_sem,
            device_id=where,
            device_id_type=MESH,
        )
        copy.start()
        pending.append(copy)
        return copy

    def spread_image(it, low, full):
        gathers = {
            k: send(low, gather_ref.at[it, k], gather_send.at[it, k], gather_recv.at[it, k], {"coil": peers[k]})
            for k in order
        }
        besides = [
            send(full, beside_ref.at[it, side], beside_send.at[it, side], beside_recv.at[it, side], {"frame": where})
            for side, where in ((0, later), (1, earlier))
        ]
        return gathers, besides

    gathers, besides = spread_image(0, low_ref.at[0], moving_ref.at[0])

    for place in range(4, 10):
        loads[place].wait()
    loads[10].wait()
    cosine = table_ref[:, :size]
    sine = table_ref[:, size:]
    forward_ref[:size, :size] = cosine
    forward_ref[:size, size:] = -sine
    forward_ref[size:, :size] = sine
    forward_ref[size:, size:] = cosine
    inverse_ref[:size, :size] = cosine
    inverse_ref[:size, size:] = sine
    inverse_ref[size:, :size] = -sine
    inverse_ref[size:, size:] = cosine

    strip = 64
    group = max(d for d in range(1, GROUP + 1) if blocks % d == 0)

    def build(block, carry):
        for first_ref, off_ref, taps_ref, into_ref in (
            (row_first_ref, row_off_ref, row_taps_ref, row_ref),
            (col_first_ref, col_off_ref, col_taps_ref, col_ref),
        ):
            first = first_ref[block] + off_ref[0, block]
            weights = taps_ref[0, block].astype(F32)
            for low in range(0, size, strip):
                distance = lax.broadcasted_iota(jnp.int32, (strip, spoke), 0) + low - first
                matrix = jnp.zeros((strip, spoke), F32)
                for tap in range(taps):
                    matrix = jnp.where(distance == tap, weights[tap : tap + 1], matrix)
                into_ref[block, low : low + strip, :] = matrix.astype(BF16)
        return carry

    lax.fori_loop(0, blocks, build, 0)
    tally_ref[...] = jnp.zeros_like(tally_ref)
    for place in range(1, 4):
        loads[place].wait()
    used = used_ref[0, 0]
    momentum = 1.0

    for it in range(ITERS):
        for k in [0] + order[::-1]:
            if k == 0:
                piece = low_ref[it]
            else:
                gathers[k].wait_recv()
                piece = gather_ref[it, k]
            piece = piece.astype(F32)
            owner = owners[k]
            at = pl.multiple_of(owner * rows, rows)
            at_below = pl.multiple_of(owner * rows + size, rows)
            map_real = maps_ref[0, 0, pl.ds(at, rows), :].astype(F32)
            map_imag = maps_ref[0, 1, pl.ds(at, rows), :].astype(F32)
            real = (map_real * piece[0] - map_imag * piece[1]).astype(BF16).astype(wire)
            imag = (map_real * piece[1] + map_imag * piece[0]).astype(BF16).astype(wire)
            stack_ref[pl.ds(at, rows), :size] = real
            stack_ref[pl.ds(at, rows), size:] = imag
            stack_ref[pl.ds(at_below, rows), :size] = imag
            stack_ref[pl.ds(at_below, rows), size:] = -real
        half = dot(table_ref[...], stack_ref[...].astype(BF16)).astype(BF16)
        kspace = dot(half, forward_ref[...]).astype(BF16)
        space_ref[:size] = kspace[:, :size]
        space_ref[size:] = kspace[:, size:]
        grid_ref[...] = jnp.zeros_like(grid_ref)

        def visit(turn, total):
            weighted = ([], [])
            sides = []
            for member in range(group):
                block = turn * group + member
                cols = col_ref[block]
                sides.append(cols)
                rows_wide = row_ref[block].astype(F32)
                across = dot(space_ref[...], cols)
                measured = samples_ref[0, 0, block].astype(F32)
                active = jnp.where(block < used, 1.0, 0.0)
                for p in range(2):
                    predicted = jnp.sum(
                        across[p * size : (p + 1) * size] * rows_wide, axis=0, keepdims=True
                    )
                    resid = (predicted - measured[p : p + 1]) * active
                    total = total + resid * resid
                    resid_low = resid.astype(BF16).astype(F32)
                    weighted[p].append((resid_low * rows_wide).astype(BF16))
            both = jnp.concatenate([jnp.concatenate(part, axis=1) for part in weighted], axis=0)
            grid_ref[...] += dot_nt(both, jnp.concatenate(sides, axis=1))
            return total

        total = lax.fori_loop(0, blocks // group, visit, jnp.zeros((1, spoke), F32))
        tally_ref[it : it + 1, :] = total
        tally_copies = []
        if it == ITERS - 1:
            tally_copies = [
                send(tally_ref, tallies_ref.at[k], tally_send.at[k], tally_recv.at[k], {"coil": peers[k]})
                for k in range(1, coils)
            ]
        grid_real = grid_ref[:size].astype(BF16)
        grid_imag = grid_ref[size:].astype(BF16)
        turned = jnp.concatenate(
            [
                jnp.concatenate([grid_real, grid_imag], axis=1),
                jnp.concatenate([-grid_imag, grid_real], axis=1),
            ],
            axis=0,
        )
        back_half = dot(table_ref[...], turned).astype(BF16)
        coil_back = dot(back_half, inverse_ref[...])
        map_real = maps_ref[0, 0].astype(F32)
        map_imag = maps_ref[0, 1].astype(F32)
        back_real = coil_back[:, :size]
        back_imag = coil_back[:, size:]
        real = map_real * back_real + map_imag * back_imag
        imag = map_real * back_imag - map_imag * back_real
        outgo_ref[it, 0] = real.astype(wire)
        outgo_ref[it, 1] = imag.astype(wire)
        incomes = {}
        for k in order:
            at = pl.multiple_of(peers[k] * rows, rows)
            incomes[k] = send(
                outgo_ref.at[it, :, pl.ds(at, rows), :],
                income_ref.at[it, k],
                income_send.at[it, k],
                income_recv.at[it, k],
                {"coil": peers[k]},
            )
        grad_ref[0] = real
        grad_ref[1] = imag

        for copy in besides:
            copy.wait_recv()
        moving = [moving_ref[it, p] for p in range(2)]
        ahead = [beside_ref[it, 1, p] - moving[p] for p in range(2)]
        behind = [moving[p] - beside_ref[it, 0, p] for p in range(2)]
        floor = smooth_floor * smooth_floor
        ahead_length = jnp.sqrt(ahead[0] * ahead[0] + ahead[1] * ahead[1] + floor)
        behind_length = jnp.sqrt(behind[0] * behind[0] + behind[1] * behind[1] + floor)
        variation = [behind[p] / behind_length - ahead[p] / ahead_length for p in range(2)]

        here = pl.multiple_of(coil * rows, rows)
        sums = [grad_ref[p, pl.ds(here, rows), :] for p in range(2)]
        for k in range(1, coils):
            incomes[k].wait_recv()
            sums = [sums[p] + income_ref[it, k, p].astype(F32) for p in range(2)]
        descent = [moving[p] - step_size * (sums[p] + tv_weight * variation[p]) for p in range(2)]
        doubled = wavelet_prox(descent, step_size * shrink_weight)
        updated = [doubled[p] * 0.5 for p in range(2)]
        following = (1.0 + math.sqrt(1.0 + 4.0 * momentum * momentum)) / 2.0
        if it == ITERS - 1:
            tiles = size // LANES
            for p in range(2):
                for tile in range(tiles):
                    image_ref[pl.ds(2 * tile + p, rows, stride=2 * tiles), :] = doubled[p][
                        :, tile * LANES : (tile + 1) * LANES
                    ]
        else:
            factor = (momentum - 1.0) / following
            for p in range(2):
                ahead_value = updated[p]
                if factor != 0.0:
                    ahead_value = ahead_value + factor * (updated[p] - current_ref[p])
                low_ref[it + 1, p] = ahead_value.astype(BF16).astype(wire)
                moving_ref[it + 1, p] = ahead_value
                current_ref[p] = updated[p]
            gathers, besides = spread_image(it + 1, low_ref.at[it + 1], moving_ref.at[it + 1])
        momentum = following

    tally = tally_ref[...]
    for k in range(1, coils):
        tally_copies[k - 1].wait_recv()
        tally = tally + tallies_ref[k]
    lane = lax.broadcasted_iota(jnp.int32, (1, ITERS), 1)
    misfit = jnp.zeros((1, ITERS), F32)
    for it in range(ITERS):
        misfit = jnp.where(lane == it, jnp.sum(tally[it : it + 1], axis=1, keepdims=True), misfit)
    misfit_ref[...] = misfit
    for copy in pending:
        copy.wait_send()


def on_device(coils, frames, table, image, coil_maps, samples, blocks_used, row_off, col_off, row_first, col_first, *taps):
    size = coil_maps.shape[3]
    blocks = samples.shape[2]
    spoke = samples.shape[4]
    rows = size // coils
    wire = BF16 if rows % 16 == 0 else F32
    row_first = jnp.transpose(row_first, (1, 0, 2))
    col_first = jnp.transpose(col_first, (1, 0, 2))
    vmem = pl.BlockSpec(memory_space=pltpu.VMEM)
    operands = (
        image,
        coil_maps,
        samples,
        blocks_used.reshape(1, 1),
        row_off,
        col_off,
        row_first,
        col_first,
        *taps,
        table,
    )
    scalars = (3, 4, 5)
    held = [
        (pltpu.SMEM if place in scalars else pltpu.VMEM)(operand.shape, operand.dtype)
        for place, operand in enumerate(operands)
    ]
    shard = (2, rows, size)
    dma = pltpu.SemaphoreType.DMA
    doubled, misfit = pl.pallas_call(
        functools.partial(kernel, coils, frames),
        out_shape=(
            jax.ShapeDtypeStruct((2 * rows * size // LANES, LANES), F32),
            jax.ShapeDtypeStruct((1, ITERS), F32),
        ),
        in_specs=[pl.BlockSpec(memory_space=pl.ANY)] * len(operands),
        out_specs=(vmem, vmem),
        scratch_shapes=held
        + [
            dma((len(operands),)),
            pltpu.VMEM((2 * size, 2 * size), BF16),
            pltpu.VMEM((2 * size, 2 * size), BF16),
            pltpu.VMEM((blocks, size, spoke), BF16),
            pltpu.VMEM((blocks, size, spoke), BF16),
            pltpu.VMEM((2 * size, 2 * size), wire),
            pltpu.VMEM((2 * size, size), BF16),
            pltpu.VMEM((2 * size, size), F32),
            pltpu.VMEM((2, size, size), F32),
            pltpu.VMEM((ITERS,) + shard, F32),
            pltpu.VMEM(shard, F32),
            pltpu.VMEM((ITERS,) + shard, wire),
            pltpu.VMEM((ITERS, coils) + shard, wire),
            pltpu.VMEM((ITERS, 2, size, size), wire),
            pltpu.VMEM((ITERS, coils) + shard, wire),
            pltpu.VMEM((ITERS, 2) + shard, F32),
            pltpu.VMEM((8, spoke), F32),
            pltpu.VMEM((coils, 8, spoke), F32),
            dma((ITERS, coils)),
            dma((ITERS, coils)),
            dma((ITERS, coils)),
            dma((ITERS, coils)),
            dma((ITERS, 2)),
            dma((ITERS, 2)),
            dma((coils,)),
            dma((coils,)),
        ],
        compiler_params=pltpu.CompilerParams(
            collective_id=0, has_side_effects=True, vmem_limit_bytes=56 * 1024 * 1024
        ),
    )(*operands)
    updated = (doubled * 0.5).reshape(rows, size // LANES, 2, LANES).transpose(0, 2, 1, 3)
    scale = 0.5 / (coils * blocks * spoke)
    return updated.reshape(image.shape), jnp.transpose(misfit * scale)


def solution(mesh):
    placed = (
        P("coil", "frame", None, None),
        P("coil", None, None, None),
        P("coil", "frame", None, None, None),
        P("frame"),
        P("frame", None),
        P("frame", None),
        P("frame", None, None),
        P("frame", None, None),
        P("frame", None, None, None),
        P("frame", None, None, None),
    )

    def run(*args):
        table = jnp.asarray(table_pair(args[1].shape[3]))
        body = functools.partial(on_device, mesh.shape["coil"], mesh.shape["frame"], table)
        return jax.shard_map(
            body,
            mesh=mesh,
            in_specs=placed,
            out_specs=(P("coil", "frame", None, None), P(None, "frame")),
            check_vma=False,
        )(*args)

    return run
```

profile of v0, /device:TPU:1, one launch (start us, length us, event | category | flops | bytes accessed | tf_op | source)
XLA Modules:
  0.0 89.9 jit_solution(5420865050584998372)
XLA Ops:
  1.3 86.2 %shard_map.122 = (f32[32,128]{1,0:T(8,128)}, f32[1,2]{1,0:T(1,128)}) custom-call(f32[8,1,2,256]{3,2,1,0:T(2,128)} %refs_0_.1, bf16[1,2,256,256]{3,2,1,0:T(8,128)(2,1)} %refs_1_.1, bf16[1,1,18,2,256]{4,3,2,1,0:T(2,128)(2,1)} %refs_2_.1, s32[1,1]{1,0:T(1,128)} %bitcast.10.refs_3_, s32[1,18]{1,0:T(1,128)} %refs_4_.1, s32[1,18]{1,0:T(1,128)} %refs_5_.1, ...), custom_call_target="tpu_custom_call" | custom-call | tf_op jit(solution)/shard_map/pallas_call | solution.py:422
  87.4 1.3 %broadcast_multiply_fusion = f32[32,128]{1,0:T(8,128)} fusion(f32[32,128]{1,0:T(8,128)} %get-tuple-element.4), kind=kLoop, calls=%fused_computation | loop fusion | flops 4096 | bytes 32768 | tf_op jit(solution)/shard_map/mul | solution.py:463
  88.8 0.0 copy-start
  88.8 0.7 copy-done
  89.4 0.5 multiply_bitcast_fusion
Async XLA Ops:
  88.8 0.7 copy-start
where the time goes:
time: 91.1 us; the launch traced here: 89.9 us
  Pallas kernels  86.2 us (95%)
  other arithmetic  1.84 us (2%)
  between operations  1.29 us (1%)
    pallas_call x1, Pallas kernels, on_device(): pl.pallas_call(functools.partial(kernel, coils, frames), out_shape=(jax.S...  86.2 us

commit v1 on v0

v1 whole, which is shorter than its diff:
```python
import functools
import math

import jax
import jax.numpy as jnp
import ml_dtypes
import numpy as np
from jax import lax
from jax.experimental import pallas as pl
from jax.experimental.pallas import tpu as pltpu
from jax.sharding import PartitionSpec as P

ITERS = 2
GROUP = 6
EARLY = 6
LANES = 128
TILE = 128
PACK = 16

step_size = 2.0
tv_weight = 0.1
smooth_floor = 0.5
shrink_weight = 0.1

F32 = jnp.float32
BF16 = jnp.bfloat16
MESH = pl.DeviceIdType.MESH


def pair_tables(order):
    counter = np.arange(order)
    angle = (counter[:, None] * counter[None, :] % order) * (2.0 * math.pi / order)
    cosine = (np.cos(angle) / math.sqrt(order)).astype(ml_dtypes.bfloat16)
    sine = (np.sin(angle) / math.sqrt(order)).astype(ml_dtypes.bfloat16)
    return np.block([[cosine, -sine], [sine, cosine]]), np.block([[cosine, sine], [-sine, cosine]])


def far_first(coils):
    across = 4 if coils % 4 == 0 else 1
    along = coils // across

    def hops(shift):
        dx, dz = shift
        return min(dx, across - dx) + min(dz, along - dz)

    shifts = [(dx, dz) for dx in range(across) for dz in range(along) if dx or dz]
    return across, along, sorted(shifts, key=hops, reverse=True)


def dot(left, right):
    return jnp.dot(left, right, preferred_element_type=F32)


def dot_nt(left, right):
    return lax.dot_general(left, right, (((1,), (1,)), ((), ())), preferred_element_type=F32)


def partner(values, axis, parity):
    size = values.shape[axis]
    return jnp.where(
        parity == 0, pltpu.roll(values, size - 1, axis), pltpu.roll(values, 1, axis)
    )


def shrink_pair(real, imag, limit):
    length = jnp.sqrt(real * real + imag * imag)
    factor = jnp.maximum(length - limit, 0.0) / jnp.maximum(length, limit)
    return real * factor, imag * factor


def wavelet_prox(fields, limit):
    shape = fields[0].shape
    row_parity = lax.broadcasted_iota(jnp.int32, shape, 0) % 2
    col_parity = lax.broadcasted_iota(jnp.int32, shape, 1) % 2
    row_sign = jnp.where(row_parity == 0, 1.0, -1.0)
    col_sign = jnp.where(col_parity == 0, 1.0, -1.0)
    parts = []
    for field in fields:
        beside = partner(field, 1, col_parity)
        col_sum = field + beside
        col_diff = (field - beside) * col_sign
        sum_below = partner(col_sum, 0, row_parity)
        diff_below = partner(col_diff, 0, row_parity)
        approx = (col_sum + sum_below) * 0.5
        horiz = (col_diff + diff_below) * 0.5
        vertical = (col_sum - sum_below) * row_sign * 0.5
        diagonal = (col_diff - diff_below) * row_sign * 0.5
        parts.append((approx, horiz, vertical, diagonal))
    real, imag = parts
    horiz = shrink_pair(real[1], imag[1], limit)
    vertical = shrink_pair(real[2], imag[2], limit)
    diagonal = shrink_pair(real[3], imag[3], limit)
    return [
        (parts[p][0] + col_sign * horiz[p] + row_sign * vertical[p] + row_sign * col_sign * diagonal[p])
        for p in range(2)
    ]


def kernel(
    coils,
    frames,
    used_ref,
    *refs,
):
    inputs = refs[:11]
    image_ref, misfit_ref = refs[11:13]
    held = refs[13:24]
    input_sem = refs[24]
    loads = []
    for place, (source, target) in enumerate(zip(inputs, held)):
        copy = pltpu.make_async_copy(source, target, input_sem.at[place])
        copy.start()
        loads.append(copy)
    run(coils, frames, loads, used_ref, *held, image_ref, misfit_ref, *refs[25:])


def run(
    coils,
    frames,
    loads,
    used_ref,
    start_ref,
    row_off_ref,
    col_off_ref,
    row_first_ref,
    col_first_ref,
    row_taps_ref,
    col_taps_ref,
    maps_ref,
    samples_ref,
    minus_ref,
    plus_ref,
    image_ref,
    misfit_ref,
    row_ref,
    col_ref,
    space_ref,
    grid_ref,
    moving_ref,
    current_ref,
    low_ref,
    gather_ref,
    outgo_ref,
    income_ref,
    beside_ref,
    tally_ref,
    tallies_ref,
    send_sem,
    recv_sem,
    beside_send,
    beside_recv,
):
    coil = lax.axis_index("coil")
    frame = lax.axis_index("frame")
    size = maps_ref.shape[2]
    blocks = samples_ref.shape[2]
    spoke = samples_ref.shape[4]
    taps = row_taps_ref.shape[2]
    rows = size // coils
    tiles = size // PACK
    window = min(TILE // PACK + 1, tiles)
    later = lax.rem(frame + 1, frames)
    earlier = lax.rem(frame + frames - 1, frames)
    across, along, shifts = far_first(coils)
    coil_x = coil // along
    coil_z = lax.rem(coil, along)
    peers = [lax.rem(coil_x + dx, across) * along + lax.rem(coil_z + dz, along) for dx, dz in shifts]

    barrier = pltpu.get_barrier_semaphore()
    for peer in peers:
        pl.semaphore_signal(barrier, inc=1, device_id={"coil": peer}, device_id_type=MESH)
    for nearby in (later, earlier):
        pl.semaphore_signal(barrier, inc=1, device_id={"frame": nearby}, device_id_type=MESH)

    loads[0].wait()
    value = [start_ref[:, 0, p, :] for p in range(2)]
    for p in range(2):
        moving_ref[0, p] = value[p]
        current_ref[p] = value[p]
    piece = jnp.concatenate(value, axis=0).astype(BF16)
    low_ref[0] = piece
    gather_ref[0, coil] = piece

    for place in range(1, 7):
        loads[place].wait()
    strip = 64

    def build(block, carry):
        for first_ref, off_ref, taps_ref, into_ref in (
            (row_first_ref, row_off_ref, row_taps_ref, row_ref),
            (col_first_ref, col_off_ref, col_taps_ref, col_ref),
        ):
            first = first_ref[block] + off_ref[0, block]
            weights = taps_ref[0, block].astype(F32)
            for low in range(0, size, strip):
                distance = lax.broadcasted_iota(jnp.int32, (strip, spoke), 0) + low - first
                matrix = jnp.zeros((strip, spoke), F32)
                for tap in range(taps):
                    matrix = jnp.where(distance == tap, weights[tap : tap + 1], matrix)
                matrix = matrix.astype(BF16)
                if into_ref is row_ref:
                    into_ref[block, low // PACK : (low + strip) // PACK] = matrix.reshape(strip // PACK, PACK, spoke)
                else:
                    into_ref[block, low : low + strip, :] = matrix
        return carry

    early = min(EARLY, blocks)
    lax.fori_loop(0, early, build, 0)
    pl.semaphore_wait(barrier, coils - 1 + 2)

    pending = []

    def send(source, target, sent, received, where):
        copy = pltpu.make_async_remote_copy(
            src_ref=source,
            dst_ref=target,
            send_sem=sent,
            recv_sem=received,
            device_id=where,
            device_id_type=MESH,
        )
        copy.start()
        return copy

    def take_all(phase, ref, sem):
        pltpu.make_async_copy(ref, ref, sem.at[phase]).wait()

    def spread_image(it):
        for peer in peers:
            send(low_ref.at[it], gather_ref.at[it, coil], send_sem.at[2 * it], recv_sem.at[2 * it], {"coil": peer})
        return [
            send(
                moving_ref.at[it], beside_ref.at[it, side], beside_send.at[it, side], beside_recv.at[it, side], {"frame": where}
            )
            for side, where in ((0, later), (1, earlier))
        ]

    besides = spread_image(0)
    pending.extend(besides)
    lax.fori_loop(early, blocks, build, 0)
    for place in range(7, 11):
        loads[place].wait()
    group = max(d for d in range(1, GROUP + 1) if blocks % d == 0)
    used = used_ref[0]
    momentum = 1.0
    others = pl.ds(0, coils - 1)

    for it in range(ITERS):
        take_all(2 * it, gather_ref.at[it, others], recv_sem)
        pieces = gather_ref[it].astype(F32)
        real, imag = pieces[:, :rows], pieces[:, rows:]
        map_real = maps_ref[0, 0].astype(F32).reshape(coils, rows, size)
        map_imag = maps_ref[0, 1].astype(F32).reshape(coils, rows, size)
        stack = jnp.concatenate(
            [
                (map_real * real - map_imag * imag).reshape(size, size).astype(BF16),
                (map_real * imag + map_imag * real).reshape(size, size).astype(BF16),
            ],
            axis=0,
        )
        half = dot(plus_ref[...], stack).astype(BF16)
        kspace = dot(jnp.concatenate([half[:size], half[size:]], axis=1), minus_ref[...]).astype(BF16)
        space_ref[:, 0] = kspace[:, :size].reshape(tiles, PACK, size)
        space_ref[:, 1] = kspace[:, size:].reshape(tiles, PACK, size)
        grid_ref[...] = jnp.zeros_like(grid_ref)

        def visit(turn, total):
            weighted = ([], [])
            sides = []
            for member in range(group):
                block = turn * group + member
                cols = col_ref[block]
                sides.append(cols)
                at = jnp.minimum(row_off_ref[0, block] // PACK, tiles - window)
                near = space_ref[pl.ds(at, window)].reshape(window * 2 * PACK, size)
                reach = dot(near, cols).reshape(window, 2, PACK, spoke)
                rows_near = row_ref[block, pl.ds(at, window)].astype(F32)
                rows_wide = row_ref[block].reshape(size, spoke).astype(F32)
                measured = samples_ref[0, 0, block].astype(F32)
                active = jnp.where(block < used, 1.0, 0.0)
                for p in range(2):
                    predicted = jnp.sum(
                        (reach[:, p] * rows_near).reshape(window * PACK, spoke), axis=0, keepdims=True
                    )
                    resid = (predicted - measured[p : p + 1]) * active
                    total = total + resid * resid
                    resid_low = resid.astype(BF16).astype(F32)
                    weighted[p].append((resid_low * rows_wide).astype(BF16))
            both = jnp.concatenate([jnp.concatenate(part, axis=1) for part in weighted], axis=0)
            grid_ref[...] += dot_nt(both, jnp.concatenate(sides, axis=1))
            return total

        total = lax.fori_loop(0, blocks // group, visit, jnp.zeros((1, spoke), F32))
        summed = jnp.sum(total, axis=1, keepdims=True)
        lane = lax.broadcasted_iota(jnp.int32, (1, LANES), 1)
        tally = jnp.where(lane == it, summed, 0.0 if it == 0 else tally)
        if it == ITERS - 1:
            tally_ref[...] = tally
            tallies_ref[coil] = tally
        spread = grid_ref[...].astype(BF16)
        back_half = dot(minus_ref[...], spread).astype(BF16)
        coil_back = dot(jnp.concatenate([back_half[:size], back_half[size:]], axis=1), plus_ref[...])
        map_real = maps_ref[0, 0].astype(F32)
        map_imag = maps_ref[0, 1].astype(F32)
        back_real = coil_back[:, :size]
        back_imag = coil_back[:, size:]
        real = (map_real * back_real + map_imag * back_imag).reshape(coils, rows, size)
        imag = (map_real * back_imag - map_imag * back_real).reshape(coils, rows, size)
        outgo_ref[it] = jnp.concatenate([real, imag], axis=1).astype(BF16)
        for peer in peers:
            send(
                outgo_ref.at[it, peer], income_ref.at[it, coil], send_sem.at[2 * it + 1], recv_sem.at[2 * it + 1], {"coil": peer}
            )
        if it == ITERS - 1:
            for peer in peers:
                send(tally_ref, tallies_ref.at[coil], send_sem.at[2 * ITERS], recv_sem.at[2 * ITERS], {"coil": peer})
        income_ref[it, coil] = outgo_ref[it, coil]

        for copy in besides:
            copy.wait_recv()
        moving = [moving_ref[it, p] for p in range(2)]
        ahead = [beside_ref[it, 1, p] - moving[p] for p in range(2)]
        behind = [moving[p] - beside_ref[it, 0, p] for p in range(2)]
        floor = smooth_floor * smooth_floor
        ahead_length = jnp.sqrt(ahead[0] * ahead[0] + ahead[1] * ahead[1] + floor)
        behind_length = jnp.sqrt(behind[0] * behind[0] + behind[1] * behind[1] + floor)
        variation = [behind[p] / behind_length - ahead[p] / ahead_length for p in range(2)]

        take_all(2 * it + 1, income_ref.at[it, others], recv_sem)
        sums = jnp.sum(income_ref[it].astype(F32), axis=0)
        descent = [
            moving[p] - step_size * (sums[p * rows : (p + 1) * rows] + tv_weight * variation[p]) for p in range(2)
        ]
        doubled = wavelet_prox(descent, step_size * shrink_weight)
        updated = [doubled[p] * 0.5 for p in range(2)]
        following = (1.0 + math.sqrt(1.0 + 4.0 * momentum * momentum)) / 2.0
        if it == ITERS - 1:
            lots = size // LANES
            for p in range(2):
                for lot in range(lots):
                    image_ref[pl.ds(2 * lot + p, rows, stride=2 * lots), :] = doubled[p][
                        :, lot * LANES : (lot + 1) * LANES
                    ]
        else:
            factor = (momentum - 1.0) / following
            value = []
            for p in range(2):
                ahead_value = updated[p]
                if factor != 0.0:
                    ahead_value = ahead_value + factor * (updated[p] - current_ref[p])
                value.append(ahead_value)
                moving_ref[it + 1, p] = ahead_value
                current_ref[p] = updated[p]
            piece = jnp.concatenate(value, axis=0).astype(BF16)
            low_ref[it + 1] = piece
            gather_ref[it + 1, coil] = piece
            besides = spread_image(it + 1)
            pending.extend(besides)
        momentum = following

    take_all(2 * ITERS, tallies_ref.at[others], recv_sem)
    misfit_ref[...] = jnp.sum(tallies_ref[...], axis=0)[:, :ITERS]
    for copy in pending:
        copy.wait_send()
    for it in range(ITERS):
        take_all(2 * it, gather_ref.at[it, others], send_sem)
        take_all(2 * it + 1, income_ref.at[it, others], send_sem)
    take_all(2 * ITERS, tallies_ref.at[others], send_sem)


def on_device(
    coils, frames, tables, image, coil_maps, samples, blocks_used, row_off, col_off, row_first, col_first, row_taps, col_taps
):
    size = coil_maps.shape[3]
    blocks = samples.shape[2]
    spoke = samples.shape[4]
    rows = size // coils
    row_first = jnp.transpose(row_first, (1, 0, 2))
    col_first = jnp.transpose(col_first, (1, 0, 2))
    vmem = pl.BlockSpec(memory_space=pltpu.VMEM)
    operands = (
        image,
        row_off,
        col_off,
        row_first,
        col_first,
        row_taps,
        col_taps,
        coil_maps,
        samples,
        *tables,
    )
    scalars = (1, 2)
    held = [
        (pltpu.SMEM if place in scalars else pltpu.VMEM)(operand.shape, operand.dtype)
        for place, operand in enumerate(operands)
    ]
    shard = (2, rows, size)
    pieces = (ITERS, coils, 2 * rows, size)
    dma = pltpu.SemaphoreType.DMA
    doubled, misfit = pl.pallas_call(
        functools.partial(kernel, coils, frames),
        out_shape=(
            jax.ShapeDtypeStruct((2 * rows * size // LANES, LANES), F32),
            jax.ShapeDtypeStruct((1, ITERS), F32),
        ),
        in_specs=[pl.BlockSpec(memory_space=pltpu.SMEM)] + [pl.BlockSpec(memory_space=pl.ANY)] * len(operands),
        out_specs=(vmem, vmem),
        scratch_shapes=held
        + [
            dma((len(operands),)),
            pltpu.VMEM((blocks, size // PACK, PACK, spoke), BF16),
            pltpu.VMEM((blocks, size, spoke), BF16),
            pltpu.VMEM((size // PACK, 2, PACK, size), BF16),
            pltpu.VMEM((2 * size, size), F32),
            pltpu.VMEM((ITERS,) + shard, F32),
            pltpu.VMEM(shard, F32),
            pltpu.VMEM((ITERS, 2 * rows, size), BF16),
            pltpu.VMEM(pieces, BF16),
            pltpu.VMEM(pieces, BF16),
            pltpu.VMEM(pieces, BF16),
            pltpu.VMEM((ITERS, 2) + shard, F32),
            pltpu.VMEM((1, LANES), F32),
            pltpu.VMEM((coils, 1, LANES), F32),
            dma((2 * ITERS + 1,)),
            dma((2 * ITERS + 1,)),
            dma((ITERS, 2)),
            dma((ITERS, 2)),
        ],
        compiler_params=pltpu.CompilerParams(
            collective_id=0, has_side_effects=True, vmem_limit_bytes=56 * 1024 * 1024
        ),
    )(blocks_used, *operands)
    updated = (doubled * 0.5).reshape(rows, size // LANES, 2, LANES).transpose(0, 2, 1, 3)
    scale = 0.5 / (coils * blocks * spoke)
    return updated.reshape(image.shape), jnp.transpose(misfit * scale)


def solution(mesh):
    placed = (
        P("coil", "frame", None, None),
        P("coil", None, None, None),
        P("coil", "frame", None, None, None),
        P("frame"),
        P("frame", None),
        P("frame", None),
        P("frame", None, None),
        P("frame", None, None),
        P("frame", None, None, None),
        P("frame", None, None, None),
    )

    def run(*args):
        tables = tuple(jnp.asarray(table) for table in pair_tables(args[1].shape[3]))
        body = functools.partial(on_device, mesh.shape["coil"], mesh.shape["frame"], tables)
        return jax.shard_map(
            body,
            mesh=mesh,
            in_specs=placed,
            out_specs=(P("coil", "frame", None, None), P(None, "frame")),
            check_vma=False,
        )(*args)

    return run
```

time: 91.1 us -> 61.5 us (0.68)
  the two profiles are of different devices: /device:TPU:1 before, /device:TPU:48 now
where the time goes in v1:
time: 61.5 us; the launch traced here: 61.2 us
  Pallas kernels  57.4 us (93%)
  other arithmetic  1.84 us (3%)
  between operations  1.29 us (2%)
  local copies, waits for them, and re-layouts  0.67 us (1%)
    pallas_call x1, Pallas kernels, on_device(): pl.pallas_call(functools.partial(kernel, coils, frames), out_shape=(jax.S...  57.4 us
    mul x1, other arithmetic, on_device(): doubled * 0.5  1.33 us

profile of v1, /device:TPU:48, one launch (start us, length us, event | category | flops | bytes accessed | tf_op | source)
XLA Modules:
  0.0 61.2 jit_solution(11174827695917591169)
XLA Ops:
  1.3 57.4 %shard_map.131 = (f32[32,128]{1,0:T(8,128)}, f32[1,2]{1,0:T(1,128)}) custom-call(s32[1]{0:T(128)S(6)} %copy.15.used_ref, f32[8,1,2,256]{3,2,1,0:T(2,128)} %refs_0_.1, s32[1,18]{1,0:T(1,128)} %refs_1_.1, s32[1,18]{1,0:T(1,128)} %refs_2_.1, s32[18,1,256]{2,1,0:T(1,128)} %bitcast.9, s32[18,1,256]{2,1,0:T(1,128)} %bitcast.10, bf16[1,18,4,256]{3,2,1,0:T(4,128)(2,1)} %refs_5_.1, ...), custom_call_target="tpu_custom_call" | custom-call | tf_op jit(solution)/shard_map/pallas_call | solution.py:401
  58.7 1.3 %broadcast_multiply_fusion = f32[32,128]{1,0:T(8,128)} fusion(f32[32,128]{1,0:T(8,128)} %get-tuple-element.4), kind=kLoop, calls=%fused_computation | loop fusion | flops 4096 | bytes 32768 | tf_op jit(solution)/shard_map/mul | solution.py:434
  60.0 0.0 copy-start
  60.0 0.7 %copy-done = f32[1,2]{1,0:T(1,128)S(1)} copy-done((f32[1,2]{1,0:T(1,128)S(1)}, f32[1,2]{1,0:T(1,128)}, u32[]{:S(2)}) %copy-start) | copy-done | bytes 32
  60.7 0.5 multiply_bitcast_fusion
Async XLA Ops:
  60.0 0.7 %copy-start = (f32[1,2]{1,0:T(1,128)S(1)}, f32[1,2]{1,0:T(1,128)}, u32[]{:S(2)}) copy-start(f32[1,2]{1,0:T(1,128)} %get-tuple-element.5) | copy-start | bytes 28

commit v2 on v1

--- a/solution.py
+++ b/solution.py
@@ -11,7 +11,7 @@
 from jax.sharding import PartitionSpec as P
 
 ITERS = 2
-GROUP = 6
+GROUP = 9
 EARLY = 6
 LANES = 128
 TILE = 128
@@ -41,7 +41,7 @@
 
     def hops(shift):
         dx, dz = shift
-        return min(dx, across - dx) + min(dz, along - dz)
+        return 2 * min(dx, across - dx) + min(dz, along - dz)
 
     shifts = [(dx, dz) for dx in range(across) for dz in range(along) if dx or dz]
     return across, along, sorted(shifts, key=hops, reverse=True)
@@ -145,8 +145,12 @@
     beside_ref,
     tally_ref,
     tallies_ref,
-    send_sem,
-    recv_sem,
+    gather_send,
+    gather_recv,
+    income_send,
+    income_recv,
+    tally_send,
+    tally_recv,
     beside_send,
     beside_recv,
 ):
@@ -159,6 +163,8 @@
     rows = size // coils
     tiles = size // PACK
     window = min(TILE // PACK + 1, tiles)
+    halves = size // LANES
+    lanes = [slice(half * LANES, (half + 1) * LANES) for half in range(halves)]
     later = lax.rem(frame + 1, frames)
     earlier = lax.rem(frame + frames - 1, frames)
     across, along, shifts = far_first(coils)
@@ -178,8 +184,9 @@
         moving_ref[0, p] = value[p]
         current_ref[p] = value[p]
     piece = jnp.concatenate(value, axis=0).astype(BF16)
-    low_ref[0] = piece
-    gather_ref[0, coil] = piece
+    for half in range(halves):
+        low_ref[0, half] = piece[:, lanes[half]]
+        gather_ref[0, coil, half] = piece[:, lanes[half]]
 
     for place in range(1, 7):
         loads[place].wait()
@@ -208,8 +215,6 @@
     lax.fori_loop(0, early, build, 0)
     pl.semaphore_wait(barrier, coils - 1 + 2)
 
-    pending = []
-
     def send(source, target, sent, received, where):
         copy = pltpu.make_async_remote_copy(
             src_ref=source,
@@ -222,12 +227,10 @@
         copy.start()
         return copy
 
-    def take_all(phase, ref, sem):
-        pltpu.make_async_copy(ref, ref, sem.at[phase]).wait()
-
-    def spread_image(it):
-        for peer in peers:
-            send(low_ref.at[it], gather_ref.at[it, coil], send_sem.at[2 * it], recv_sem.at[2 * it], {"coil": peer})
+    def take_all(ref, sem):
+        pltpu.make_async_copy(ref, ref, sem).wait()
+
+    def greet(it):
         return [
             send(
                 moving_ref.at[it], beside_ref.at[it, side], beside_send.at[it, side], beside_recv.at[it, side], {"frame": where}
@@ -235,8 +238,10 @@
             for side, where in ((0, later), (1, earlier))
         ]
 
-    besides = spread_image(0)
-    pending.extend(besides)
+    for peer in peers:
+        send(low_ref.at[0], gather_ref.at[0, coil], gather_send.at[0], gather_recv.at[0, 0], {"coil": peer})
+    besides = greet(0)
+    pending = list(besides)
     lax.fori_loop(early, blocks, build, 0)
     for place in range(7, 11):
         loads[place].wait()
@@ -245,24 +250,35 @@
     momentum = 1.0
     others = pl.ds(0, coils - 1)
 
-    for it in range(ITERS):
-        take_all(2 * it, gather_ref.at[it, others], recv_sem)
-        pieces = gather_ref[it].astype(F32)
+    def first_half(pieces, cols):
         real, imag = pieces[:, :rows], pieces[:, rows:]
-        map_real = maps_ref[0, 0].astype(F32).reshape(coils, rows, size)
-        map_imag = maps_ref[0, 1].astype(F32).reshape(coils, rows, size)
+        width = real.shape[-1]
+        map_real = maps_ref[0, 0, :, cols].astype(F32).reshape(coils, rows, width)
+        map_imag = maps_ref[0, 1, :, cols].astype(F32).reshape(coils, rows, width)
         stack = jnp.concatenate(
             [
-                (map_real * real - map_imag * imag).reshape(size, size).astype(BF16),
-                (map_real * imag + map_imag * real).reshape(size, size).astype(BF16),
+                (map_real * real - map_imag * imag).reshape(size, width).astype(BF16),
+                (map_real * imag + map_imag * real).reshape(size, width).astype(BF16),
             ],
             axis=0,
         )
-        half = dot(plus_ref[...], stack).astype(BF16)
-        kspace = dot(jnp.concatenate([half[:size], half[size:]], axis=1), minus_ref[...]).astype(BF16)
+        return dot(plus_ref[...], stack).astype(BF16)
+
+    for it in range(ITERS):
+        if it == 0:
+            take_all(gather_ref.at[it, others], gather_recv.at[it, 0])
+            pieces = gather_ref[it].astype(F32)
+            pieces = jnp.concatenate([pieces[:, half] for half in range(halves)], axis=-1)
+            half_sum = first_half(pieces, slice(0, size))
+        else:
+            parts = []
+            for half in range(halves):
+                take_all(gather_ref.at[it, others, half], gather_recv.at[it, half])
+                parts.append(first_half(gather_ref[it, :, half].astype(F32), lanes[half]))
+            half_sum = jnp.concatenate(parts, axis=1)
+        kspace = dot(jnp.concatenate([half_sum[:size], half_sum[size:]], axis=1), minus_ref[...]).astype(BF16)
         space_ref[:, 0] = kspace[:, :size].reshape(tiles, PACK, size)
         space_ref[:, 1] = kspace[:, size:].reshape(tiles, PACK, size)
-        grid_ref[...] = jnp.zeros_like(grid_ref)
 
         def visit(turn, total):
             weighted = ([], [])
@@ -287,10 +303,19 @@
                     resid_low = resid.astype(BF16).astype(F32)
                     weighted[p].append((resid_low * rows_wide).astype(BF16))
             both = jnp.concatenate([jnp.concatenate(part, axis=1) for part in weighted], axis=0)
-            grid_ref[...] += dot_nt(both, jnp.concatenate(sides, axis=1))
+            spread = dot_nt(both, jnp.concatenate(sides, axis=1))
+            if group == blocks:
+                grid_ref[...] = spread
+            else:
+                grid_ref[...] += spread
             return total
 
-        total = lax.fori_loop(0, blocks // group, visit, jnp.zeros((1, spoke), F32))
+        total = jnp.zeros((1, spoke), F32)
+        if group == blocks:
+            total = visit(0, total)
+        else:
+            grid_ref[...] = jnp.zeros_like(grid_ref)
+            total = lax.fori_loop(0, blocks // group, visit, total)
         summed = jnp.sum(total, axis=1, keepdims=True)
         lane = lax.broadcasted_iota(jnp.int32, (1, LANES), 1)
         tally = jnp.where(lane == it, summed, 0.0 if it == 0 else tally)
@@ -299,22 +324,29 @@
             tallies_ref[coil] = tally
         spread = grid_ref[...].astype(BF16)
         back_half = dot(minus_ref[...], spread).astype(BF16)
-        coil_back = dot(jnp.concatenate([back_half[:size], back_half[size:]], axis=1), plus_ref[...])
-        map_real = maps_ref[0, 0].astype(F32)
-        map_imag = maps_ref[0, 1].astype(F32)
-        back_real = coil_back[:, :size]
-        back_imag = coil_back[:, size:]
-        real = (map_real * back_real + map_imag * back_imag).reshape(coils, rows, size)
-        imag = (map_real * back_imag - map_imag * back_real).reshape(coils, rows, size)
-        outgo_ref[it] = jnp.concatenate([real, imag], axis=1).astype(BF16)
-        for peer in peers:
-            send(
-                outgo_ref.at[it, peer], income_ref.at[it, coil], send_sem.at[2 * it + 1], recv_sem.at[2 * it + 1], {"coil": peer}
-            )
+        back_half = jnp.concatenate([back_half[:size], back_half[size:]], axis=1)
+        for half in range(halves):
+            beyond = slice(size + half * LANES, size + (half + 1) * LANES)
+            coil_back = dot(back_half, jnp.concatenate([plus_ref[:, lanes[half]], plus_ref[:, beyond]], axis=1))
+            map_real = maps_ref[0, 0, :, lanes[half]].astype(F32)
+            map_imag = maps_ref[0, 1, :, lanes[half]].astype(F32)
+            back_real = coil_back[:, :LANES]
+            back_imag = coil_back[:, LANES:]
+            real = (map_real * back_real + map_imag * back_imag).reshape(coils, rows, LANES)
+            imag = (map_real * back_imag - map_imag * back_real).reshape(coils, rows, LANES)
+            outgo_ref[it, half] = jnp.concatenate([real, imag], axis=1).astype(BF16)
+            for peer in peers:
+                send(
+                    outgo_ref.at[it, half, peer],
+                    income_ref.at[it, half, coil],
+                    income_send.at[it, half],
+                    income_recv.at[it, half],
+                    {"coil": peer},
+                )
+            income_ref[it, half, coil] = outgo_ref[it, half, coil]
         if it == ITERS - 1:
             for peer in peers:
-                send(tally_ref, tallies_ref.at[coil], send_sem.at[2 * ITERS], recv_sem.at[2 * ITERS], {"coil": peer})
-        income_ref[it, coil] = outgo_ref[it, coil]
+                send(tally_ref, tallies_ref.at[coil], tally_send.at[0], tally_recv.at[0], {"coil": peer})
 
         for copy in besides:
             copy.wait_recv()
@@ -325,47 +357,56 @@
         ahead_length = jnp.sqrt(ahead[0] * ahead[0] + ahead[1] * ahead[1] + floor)
         behind_length = jnp.sqrt(behind[0] * behind[0] + behind[1] * behind[1] + floor)
         variation = [behind[p] / behind_length - ahead[p] / ahead_length for p in range(2)]
-
-        take_all(2 * it + 1, income_ref.at[it, others], recv_sem)
-        sums = jnp.sum(income_ref[it].astype(F32), axis=0)
-        descent = [
-            moving[p] - step_size * (sums[p * rows : (p + 1) * rows] + tv_weight * variation[p]) for p in range(2)
-        ]
-        doubled = wavelet_prox(descent, step_size * shrink_weight)
-        updated = [doubled[p] * 0.5 for p in range(2)]
         following = (1.0 + math.sqrt(1.0 + 4.0 * momentum * momentum)) / 2.0
-        if it == ITERS - 1:
-            lots = size // LANES
-            for p in range(2):
-                for lot in range(lots):
-                    image_ref[pl.ds(2 * lot + p, rows, stride=2 * lots), :] = doubled[p][
-                        :, lot * LANES : (lot + 1) * LANES
-                    ]
-        else:
-            factor = (momentum - 1.0) / following
+        factor = (momentum - 1.0) / following
+
+        for half in range(halves):
+            part = lanes[half]
+            take_all(income_ref.at[it, half, others], income_recv.at[it, half])
+            sums = jnp.sum(income_ref[it, half].astype(F32), axis=0)
+            descent = [
+                moving[p][:, part] - step_size * (sums[p * rows : (p + 1) * rows] + tv_weight * variation[p][:, part])
+                for p in range(2)
+            ]
+            doubled = wavelet_prox(descent, step_size * shrink_weight)
+            if it == ITERS - 1:
+                for p in range(2):
+                    image_ref[pl.ds(2 * half + p, rows, stride=2 * halves), :] = doubled[p]
+                continue
             value = []
             for p in range(2):
-                ahead_value = updated[p]
+                updated = doubled[p] * 0.5
+                ahead_value = updated
                 if factor != 0.0:
-                    ahead_value = ahead_value + factor * (updated[p] - current_ref[p])
+                    ahead_value = ahead_value + factor * (updated - current_ref[p, :, part])
                 value.append(ahead_value)
-                moving_ref[it + 1, p] = ahead_value
-                current_ref[p] = updated[p]
+                moving_ref[it + 1, p, :, part] = ahead_value
+                current_ref[p, :, part] = updated
             piece = jnp.concatenate(value, axis=0).astype(BF16)
-            low_ref[it + 1] = piece
-            gather_ref[it + 1, coil] = piece
-            besides = spread_image(it + 1)
+            low_ref[it + 1, half] = piece
+            gather_ref[it + 1, coil, half] = piece
+            for peer in peers:
+                send(
+                    low_ref.at[it + 1, half],
+                    gather_ref.at[it + 1, coil, half],
+                    gather_send.at[it + 1],
+                    gather_recv.at[it + 1, half],
+                    {"coil": peer},
+                )
+        if it < ITERS - 1:
+            besides = greet(it + 1)
             pending.extend(besides)
         momentum = following
 
-    take_all(2 * ITERS, tallies_ref.at[others], recv_sem)
+    take_all(tallies_ref.at[others], tally_recv.at[0])
     misfit_ref[...] = jnp.sum(tallies_ref[...], axis=0)[:, :ITERS]
     for copy in pending:
         copy.wait_send()
     for it in range(ITERS):
-        take_all(2 * it, gather_ref.at[it, others], send_sem)
-        take_all(2 * it + 1, income_ref.at[it, others], send_sem)
-    take_all(2 * ITERS, tallies_ref.at[others], send_sem)
+        take_all(gather_ref.at[it, others], gather_send.at[it])
+        for half in range(halves):
+            take_all(income_ref.at[it, half, others], income_send.at[it, half])
+    take_all(tallies_ref.at[others], tally_send.at[0])
 
 
 def on_device(
@@ -396,13 +437,13 @@
         for place, operand in enumerate(operands)
     ]
     shard = (2, rows, size)
-    pieces = (ITERS, coils, 2 * rows, size)
+    halves = size // LANES
     dma = pltpu.SemaphoreType.DMA
     doubled, misfit = pl.pallas_call(
         functools.partial(kernel, coils, frames),
         out_shape=(
-            jax.ShapeDtypeStruct((2 * rows * size // LANES, LANES), F32),
-            jax.ShapeDtypeStruct((1, ITERS), F32),
+            pltpu.VMEM((2 * rows * size // LANES, LANES), F32),
+            pltpu.VMEM((1, ITERS), F32),
         ),
         in_specs=[pl.BlockSpec(memory_space=pltpu.SMEM)] + [pl.BlockSpec(memory_space=pl.ANY)] * len(operands),
         out_specs=(vmem, vmem),
@@ -415,15 +456,19 @@
             pltpu.VMEM((2 * size, size), F32),
             pltpu.VMEM((ITERS,) + shard, F32),
             pltpu.VMEM(shard, F32),
-            pltpu.VMEM((ITERS, 2 * rows, size), BF16),
-            pltpu.VMEM(pieces, BF16),
-            pltpu.VMEM(pieces, BF16),
-            pltpu.VMEM(pieces, BF16),
+            pltpu.VMEM((ITERS, halves, 2 * rows, LANES), BF16),
+            pltpu.VMEM((ITERS, coils, halves, 2 * rows, LANES), BF16),
+            pltpu.VMEM((ITERS, halves, coils, 2 * rows, LANES), BF16),
+            pltpu.VMEM((ITERS, halves, coils, 2 * rows, LANES), BF16),
             pltpu.VMEM((ITERS, 2) + shard, F32),
             pltpu.VMEM((1, LANES), F32),
             pltpu.VMEM((coils, 1, LANES), F32),
-            dma((2 * ITERS + 1,)),
-            dma((2 * ITERS + 1,)),
+            dma((ITERS,)),
+            dma((ITERS, halves)),
+            dma((ITERS, halves)),
+            dma((ITERS, halves)),
+            dma((1,)),
+            dma((1,)),
             dma((ITERS, 2)),
             dma((ITERS, 2)),
         ],

time: 61.5 us -> 55.8 us (0.907)
  the two profiles are of different devices: /device:TPU:48 before, /device:TPU:16 now
where the time goes in v2:
time: 55.8 us; the launch traced here: 55.6 us
  Pallas kernels  53.2 us (95%)
  between operations  1.29 us (2%)
  other arithmetic  1.12 us (2%)
    pallas_call x1, Pallas kernels, on_device(): pl.pallas_call(functools.partial(kernel, coils, frames), out_shape=(pltpu...  53.2 us

profile of v2, /device:TPU:16, one launch (start us, length us, event | category | flops | bytes accessed | tf_op | source)
XLA Modules:
  0.0 55.6 jit_solution(6470462225706379191)
XLA Ops:
  1.3 53.2 %shard_map.131 = (f32[32,128]{1,0:T(8,128)S(1)}, f32[1,2]{1,0:T(1,128)S(1)}) custom-call(s32[1]{0:T(128)S(6)} %copy.15.used_ref, f32[8,1,2,256]{3,2,1,0:T(2,128)} %refs_0_.1, s32[1,18]{1,0:T(1,128)} %refs_1_.1, s32[1,18]{1,0:T(1,128)} %refs_2_.1, s32[18,1,256]{2,1,0:T(1,128)} %bitcast.9, s32[18,1,256]{2,1,0:T(1,128)} %bitcast.10, ...), custom_call_target="tpu_custom_call" | custom-call | tf_op jit(solution)/shard_map/pallas_call | solution.py:442
  54.5 0.6 %broadcast_multiply_fusion = f32[32,128]{1,0:T(8,128)} fusion(f32[32,128]{1,0:T(8,128)S(1)} %get-tuple-element.4), kind=kLoop, calls=%fused_computation | loop fusion | flops 4096 | bytes 32768 | tf_op jit(solution)/shard_map/mul | solution.py:479
  55.1 0.5 multiply_bitcast_fusion

commit v3 on v2

--- a/solution.py
+++ b/solution.py
@@ -13,6 +13,7 @@
 ITERS = 2
 GROUP = 9
 EARLY = 6
+GATED = (True, True, True, False)
 LANES = 128
 TILE = 128
 PACK = 16
@@ -106,11 +107,11 @@
     image_ref, misfit_ref = refs[11:13]
     held = refs[13:24]
     input_sem = refs[24]
-    loads = []
-    for place, (source, target) in enumerate(zip(inputs, held)):
-        copy = pltpu.make_async_copy(source, target, input_sem.at[place])
-        copy.start()
-        loads.append(copy)
+    loads = [
+        pltpu.make_async_copy(source, target, input_sem.at[place])
+        for place, (source, target) in enumerate(zip(inputs, held))
+    ]
+    loads[0].start()
     run(coils, frames, loads, used_ref, *held, image_ref, misfit_ref, *refs[25:])
 
 
@@ -153,6 +154,7 @@
     tally_recv,
     beside_send,
     beside_recv,
+    turn_sem,
 ):
     coil = lax.axis_index("coil")
     frame = lax.axis_index("frame")
@@ -177,6 +179,8 @@
         pl.semaphore_signal(barrier, inc=1, device_id={"coil": peer}, device_id_type=MESH)
     for nearby in (later, earlier):
         pl.semaphore_signal(barrier, inc=1, device_id={"frame": nearby}, device_id_type=MESH)
+    for load in loads[1:]:
+        load.start()
 
     loads[0].wait()
     value = [start_ref[:, 0, p, :] for p in range(2)]
@@ -230,6 +234,22 @@
     def take_all(ref, sem):
         pltpu.make_async_copy(ref, ref, sem).wait()
 
+    leads = lax.rem(frame, 2) == 0
+
+    def take_turn(phase):
+        if GATED[phase]:
+
+            @pl.when(jnp.logical_not(leads))
+            def _():
+                pl.semaphore_wait(turn_sem.at[phase], 1)
+
+    def pass_turn(phase):
+        if GATED[phase]:
+
+            @pl.when(leads)
+            def _():
+                pl.semaphore_signal(turn_sem.at[phase], inc=1, device_id={"frame": later}, device_id_type=MESH)
+
     def greet(it):
         return [
             send(
@@ -238,17 +258,20 @@
             for side, where in ((0, later), (1, earlier))
         ]
 
+    take_turn(0)
     for peer in peers:
         send(low_ref.at[0], gather_ref.at[0, coil], gather_send.at[0], gather_recv.at[0, 0], {"coil": peer})
     besides = greet(0)
     pending = list(besides)
     lax.fori_loop(early, blocks, build, 0)
+    others = pl.ds(0, coils - 1)
+    take_all(gather_ref.at[0, others], gather_send.at[0])
+    pass_turn(0)
     for place in range(7, 11):
         loads[place].wait()
     group = max(d for d in range(1, GROUP + 1) if blocks % d == 0)
     used = used_ref[0]
     momentum = 1.0
-    others = pl.ds(0, coils - 1)
 
     def first_half(pieces, cols):
         real, imag = pieces[:, :rows], pieces[:, rows:]
@@ -335,6 +358,8 @@
             real = (map_real * back_real + map_imag * back_imag).reshape(coils, rows, LANES)
             imag = (map_real * back_imag - map_imag * back_real).reshape(coils, rows, LANES)
             outgo_ref[it, half] = jnp.concatenate([real, imag], axis=1).astype(BF16)
+            if half == 0:
+                take_turn(2 * it + 1)
             for peer in peers:
                 send(
                     outgo_ref.at[it, half, peer],
@@ -348,6 +373,9 @@
             for peer in peers:
                 send(tally_ref, tallies_ref.at[coil], tally_send.at[0], tally_recv.at[0], {"coil": peer})
 
+        for half in range(halves):
+            take_all(income_ref.at[it, half, others], income_send.at[it, half])
+        pass_turn(2 * it + 1)
         for copy in besides:
             copy.wait_recv()
         moving = [moving_ref[it, p] for p in range(2)]
@@ -385,6 +413,8 @@
             piece = jnp.concatenate(value, axis=0).astype(BF16)
             low_ref[it + 1, half] = piece
             gather_ref[it + 1, coil, half] = piece
+            if half == 0:
+                take_turn(2 * it + 2)
             for peer in peers:
                 send(
                     low_ref.at[it + 1, half],
@@ -396,16 +426,14 @@
         if it < ITERS - 1:
             besides = greet(it + 1)
             pending.extend(besides)
+            take_all(gather_ref.at[it + 1, others], gather_send.at[it + 1])
+            pass_turn(2 * it + 2)
         momentum = following
 
     take_all(tallies_ref.at[others], tally_recv.at[0])
     misfit_ref[...] = jnp.sum(tallies_ref[...], axis=0)[:, :ITERS]
     for copy in pending:
         copy.wait_send()
-    for it in range(ITERS):
-        take_all(gather_ref.at[it, others], gather_send.at[it])
-        for half in range(halves):
-            take_all(income_ref.at[it, half, others], income_send.at[it, half])
     take_all(tallies_ref.at[others], tally_send.at[0])
 
 
@@ -471,6 +499,7 @@
             dma((1,)),
             dma((ITERS, 2)),
             dma((ITERS, 2)),
+            pltpu.SemaphoreType.REGULAR((2 * ITERS,)),
         ],
         compiler_params=pltpu.CompilerParams(
             collective_id=0, has_side_effects=True, vmem_limit_bytes=56 * 1024 * 1024

time: 55.8 us -> 56.4 us (1.011)
  the two profiles are of different devices: /device:TPU:16 before, /device:TPU:1 now
where the time goes in v3:
time: 56.4 us; the launch traced here: 56.1 us
  Pallas kernels  53.7 us (95%)
  between operations  1.29 us (2%)
  other arithmetic  1.12 us (2%)
    pallas_call x1, Pallas kernels, on_device(): pl.pallas_call(functools.partial(kernel, coils, frames), out_shape=(pltpu...  53.7 us

profile of v3, /device:TPU:1, one launch (start us, length us, event | category | flops | bytes accessed | tf_op | source)
XLA Modules:
  0.0 56.1 jit_solution(11884292347702045364)
XLA Ops:
  1.3 53.7 %shard_map.131 = (f32[32,128]{1,0:T(8,128)S(1)}, f32[1,2]{1,0:T(1,128)S(1)}) custom-call(s32[1]{0:T(128)S(6)} %copy.15.used_ref, f32[8,1,2,256]{3,2,1,0:T(2,128)} %refs_0_.1, s32[1,18]{1,0:T(1,128)} %refs_1_.1, s32[1,18]{1,0:T(1,128)} %refs_2_.1, s32[18,1,256]{2,1,0:T(1,128)} %bitcast.9, s32[18,1,256]{2,1,0:T(1,128)} %bitcast.10, ...), custom_call_target="tpu_custom_call" | custom-call | tf_op jit(solution)/shard_map/pallas_call | solution.py:470
  55.0 0.6 %broadcast_multiply_fusion = f32[32,128]{1,0:T(8,128)} fusion(f32[32,128]{1,0:T(8,128)S(1)} %get-tuple-element.4), kind=kLoop, calls=%fused_computation | loop fusion | flops 4096 | bytes 32768 | tf_op jit(solution)/shard_map/mul | solution.py:508
  55.6 0.5 multiply_bitcast_fusion

commit v4 on v3

--- a/solution.py
+++ b/solution.py
@@ -259,14 +259,18 @@
         ]
 
     take_turn(0)
-    for peer in peers:
-        send(low_ref.at[0], gather_ref.at[0, coil], gather_send.at[0], gather_recv.at[0, 0], {"coil": peer})
+    lead = (coils - 1) // 2
+    for turn, peer in enumerate(peers):
+        send(
+            low_ref.at[0], gather_ref.at[0, coil], gather_send.at[0, int(turn >= lead)], gather_recv.at[0, 0], {"coil": peer}
+        )
     besides = greet(0)
     pending = list(besides)
     lax.fori_loop(early, blocks, build, 0)
     others = pl.ds(0, coils - 1)
-    take_all(gather_ref.at[0, others], gather_send.at[0])
+    take_all(gather_ref.at[0, pl.ds(0, lead)], gather_send.at[0, 0])
     pass_turn(0)
+    take_all(gather_ref.at[0, pl.ds(0, coils - 1 - lead)], gather_send.at[0, 1])
     for place in range(7, 11):
         loads[place].wait()
     group = max(d for d in range(1, GROUP + 1) if blocks % d == 0)
@@ -375,7 +379,8 @@
 
         for half in range(halves):
             take_all(income_ref.at[it, half, others], income_send.at[it, half])
-        pass_turn(2 * it + 1)
+            if half == 0:
+                pass_turn(2 * it + 1)
         for copy in besides:
             copy.wait_recv()
         moving = [moving_ref[it, p] for p in range(2)]
@@ -419,15 +424,17 @@
                 send(
                     low_ref.at[it + 1, half],
                     gather_ref.at[it + 1, coil, half],
-                    gather_send.at[it + 1],
+                    gather_send.at[it + 1, half],
                     gather_recv.at[it + 1, half],
                     {"coil": peer},
                 )
         if it < ITERS - 1:
             besides = greet(it + 1)
             pending.extend(besides)
-            take_all(gather_ref.at[it + 1, others], gather_send.at[it + 1])
-            pass_turn(2 * it + 2)
+            for half in range(halves):
+                take_all(gather_ref.at[it + 1, others, half], gather_send.at[it + 1, half])
+                if half == 0:
+                    pass_turn(2 * it + 2)
         momentum = following
 
     take_all(tallies_ref.at[others], tally_recv.at[0])
@@ -491,7 +498,7 @@
             pltpu.VMEM((ITERS, 2) + shard, F32),
             pltpu.VMEM((1, LANES), F32),
             pltpu.VMEM((coils, 1, LANES), F32),
-            dma((ITERS,)),
+            dma((ITERS, max(2, halves))),
             dma((ITERS, halves)),
             dma((ITERS, halves)),
             dma((ITERS, halves)),

time: 56.4 us -> 56.7 us (level)
  no operation moved by 1% of the time
where the time goes in v4:
time: 56.7 us; the launch traced here: 56.6 us
  Pallas kernels  54.2 us (96%)
  between operations  1.29 us (2%)
  other arithmetic  1.12 us (2%)
    pallas_call x1, Pallas kernels, on_device(): pl.pallas_call(functools.partial(kernel, coils, frames), out_shape=(pltpu...  54.2 us

profile of v4, /device:TPU:1, one launch (start us, length us, event | category | flops | bytes accessed | tf_op | source)
XLA Modules:
  0.0 56.6 jit_solution(11556924493006820120)
XLA Ops:
  1.3 54.2 %shard_map.131 = (f32[32,128]{1,0:T(8,128)S(1)}, f32[1,2]{1,0:T(1,128)S(1)}) custom-call(s32[1]{0:T(128)S(6)} %copy.15.used_ref, f32[8,1,2,256]{3,2,1,0:T(2,128)} %refs_0_.1, s32[1,18]{1,0:T(1,128)} %refs_1_.1, s32[1,18]{1,0:T(1,128)} %refs_2_.1, s32[18,1,256]{2,1,0:T(1,128)} %bitcast.9, s32[18,1,256]{2,1,0:T(1,128)} %bitcast.10, ...), custom_call_target="tpu_custom_call" | custom-call | tf_op jit(solution)/shard_map/pallas_call | solution.py:477
  55.5 0.6 %broadcast_multiply_fusion = f32[32,128]{1,0:T(8,128)} fusion(f32[32,128]{1,0:T(8,128)S(1)} %get-tuple-element.4), kind=kLoop, calls=%fused_computation | loop fusion | flops 4096 | bytes 32768 | tf_op jit(solution)/shard_map/mul | solution.py:515
  56.1 0.5 multiply_bitcast_fusion

commit v5 on v2

--- a/solution.py
+++ b/solution.py
@@ -12,7 +12,8 @@
 
 ITERS = 2
 GROUP = 9
-EARLY = 6
+RELAYED = 2
+REMOTE = 3
 LANES = 128
 TILE = 128
 PACK = 16
@@ -99,26 +100,24 @@
 def kernel(
     coils,
     frames,
-    used_ref,
     *refs,
 ):
-    inputs = refs[:11]
-    image_ref, misfit_ref = refs[11:13]
-    held = refs[13:24]
-    input_sem = refs[24]
-    loads = []
-    for place, (source, target) in enumerate(zip(inputs, held)):
-        copy = pltpu.make_async_copy(source, target, input_sem.at[place])
-        copy.start()
-        loads.append(copy)
-    run(coils, frames, loads, used_ref, *held, image_ref, misfit_ref, *refs[25:])
+    inputs = refs[:12]
+    image_ref, misfit_ref = refs[12:14]
+    held = refs[14:26]
+    input_sem = refs[26]
+    loads = [
+        pltpu.make_async_copy(source, target, input_sem.at[place])
+        for place, (source, target) in enumerate(zip(inputs, held))
+    ]
+    loads[0].start()
+    run(coils, frames, loads, *held, image_ref, misfit_ref, *refs[27:])
 
 
 def run(
     coils,
     frames,
     loads,
-    used_ref,
     start_ref,
     row_off_ref,
     col_off_ref,
@@ -130,6 +129,7 @@
     samples_ref,
     minus_ref,
     plus_ref,
+    used_ref,
     image_ref,
     misfit_ref,
     row_ref,
@@ -145,6 +145,8 @@
     beside_ref,
     tally_ref,
     tallies_ref,
+    first_send,
+    first_recv,
     gather_send,
     gather_recv,
     income_send,
@@ -153,6 +155,8 @@
     tally_recv,
     beside_send,
     beside_recv,
+    ready_sem,
+    relay_sem,
 ):
     coil = lax.axis_index("coil")
     frame = lax.axis_index("frame")
@@ -173,10 +177,21 @@
     peers = [lax.rem(coil_x + dx, across) * along + lax.rem(coil_z + dz, along) for dx, dz in shifts]
 
     barrier = pltpu.get_barrier_semaphore()
-    for peer in peers:
-        pl.semaphore_signal(barrier, inc=1, device_id={"coil": peer}, device_id_type=MESH)
+    depths = [lax.rem(coil_z + dz, along) for _, dz in shifts]
+
+    def signal(sem, where):
+        pl.semaphore_signal(sem, inc=1, device_id=where, device_id_type=MESH)
+
+    for peer, depth in zip(peers, depths):
+
+        @pl.when(depth >= coil_z)
+        def _():
+            signal(barrier, {"coil": peer})
+
     for nearby in (later, earlier):
-        pl.semaphore_signal(barrier, inc=1, device_id={"frame": nearby}, device_id_type=MESH)
+        signal(barrier, {"frame": nearby})
+    for load in loads[1:]:
+        load.start()
 
     loads[0].wait()
     value = [start_ref[:, 0, p, :] for p in range(2)]
@@ -188,8 +203,13 @@
         low_ref[0, half] = piece[:, lanes[half]]
         gather_ref[0, coil, half] = piece[:, lanes[half]]
 
-    for place in range(1, 7):
-        loads[place].wait()
+    pl.semaphore_wait(barrier, across * coil_z + across - 1 + 2)
+    for peer, depth in zip(peers, depths):
+
+        @pl.when(depth < coil_z)
+        def _():
+            signal(ready_sem.at[coil_z], {"coil": peer})
+
     strip = 64
 
     def build(block, carry):
@@ -211,10 +231,6 @@
                     into_ref[block, low : low + strip, :] = matrix
         return carry
 
-    early = min(EARLY, blocks)
-    lax.fori_loop(0, early, build, 0)
-    pl.semaphore_wait(barrier, coils - 1 + 2)
-
     def send(source, target, sent, received, where):
         copy = pltpu.make_async_remote_copy(
             src_ref=source,
@@ -238,17 +254,97 @@
             for side, where in ((0, later), (1, earlier))
         ]
 
-    for peer in peers:
-        send(low_ref.at[0], gather_ref.at[0, coil], gather_send.at[0], gather_recv.at[0, 0], {"coil": peer})
+    def send_first(peer, depth):
+        send(low_ref.at[0], gather_ref.at[0, coil], first_send.at[depth], first_recv.at[coil_z], {"coil": peer})
+
+    for peer, depth in zip(peers, depths):
+
+        @pl.when(depth <= coil_z)
+        def _():
+            send_first(peer, depth)
+
     besides = greet(0)
     pending = list(besides)
-    lax.fori_loop(early, blocks, build, 0)
-    for place in range(7, 11):
+    for place in range(1, 7):
         loads[place].wait()
+    lax.fori_loop(0, blocks, build, 0)
+    for place in range(7, 12):
+        loads[place].wait()
+
+    def apart(one, other):
+        return min((one - other) % along, (other - one) % along)
+
+    remote = {
+        depth: [low for low in range(1, depth) if apart(low, depth) >= REMOTE] for depth in range(along - RELAYED, along)
+    }
+    others = pl.ds(0, coils - 1)
+    seen = []
+    for depth in range(1, along):
+
+        @pl.when(coil_z < depth)
+        def _():
+            pl.semaphore_wait(ready_sem.at[depth], across)
+
+        near = coil_z < depth
+        for low in remote.get(depth, []):
+            near = jnp.logical_and(near, coil_z != low)
+
+        @pl.when(near)
+        def _():
+            for dx in sorted(range(across), key=lambda dx: -min(dx, across - dx)):
+                send_first(lax.rem(coil_x + dx, across) * along + depth, depth)
+
+        if remote.get(depth):
+
+            @pl.when(coil_z == 0)
+            def _():
+                for low in remote[depth]:
+                    if low not in seen:
+                        take_all(gather_ref.at[0, pl.ds(0, across)], first_recv.at[low])
+                        seen.append(low)
+                    for column in range(across):
+                        held = gather_ref.at[0, column * along + low]
+                        send(held, held, relay_sem.at[0], first_recv.at[low], {"coil": coil_x * along + depth})
+
+    for depth in range(along):
+
+        @pl.when(coil_z == depth)
+        def _():
+            take_all(gather_ref.at[0, pl.ds(0, across - 1)], first_recv.at[depth])
+
+        missing = coil_z != depth
+        if depth in seen:
+            missing = jnp.logical_and(missing, coil_z != 0)
+
+        @pl.when(missing)
+        def _():
+            take_all(gather_ref.at[0, pl.ds(0, across)], first_recv.at[depth])
+
+    def drain_first():
+        for depth in range(along):
+
+            @pl.when(coil_z == depth)
+            def _():
+                take_all(gather_ref.at[0, pl.ds(0, across - 1)], first_send.at[depth])
+
+            sent = coil_z != depth
+            for low in remote.get(depth, []):
+                sent = jnp.logical_and(sent, coil_z != low)
+
+            @pl.when(sent)
+            def _():
+                take_all(gather_ref.at[0, pl.ds(0, across)], first_send.at[depth])
+
+        relays = across * sum(len(lows) for lows in remote.values())
+        if relays:
+
+            @pl.when(coil_z == 0)
+            def _():
+                take_all(gather_ref.at[0, pl.ds(0, relays)], relay_sem.at[0])
+
     group = max(d for d in range(1, GROUP + 1) if blocks % d == 0)
     used = used_ref[0]
     momentum = 1.0
-    others = pl.ds(0, coils - 1)
 
     def first_half(pieces, cols):
         real, imag = pieces[:, :rows], pieces[:, rows:]
@@ -266,7 +362,6 @@
 
     for it in range(ITERS):
         if it == 0:
-            take_all(gather_ref.at[it, others], gather_recv.at[it, 0])
             pieces = gather_ref[it].astype(F32)
             pieces = jnp.concatenate([pieces[:, half] for half in range(halves)], axis=-1)
             half_sum = first_half(pieces, slice(0, size))
@@ -348,6 +443,10 @@
             for peer in peers:
                 send(tally_ref, tallies_ref.at[coil], tally_send.at[0], tally_recv.at[0], {"coil": peer})
 
+        if it == 0:
+            drain_first()
+        for half in range(halves):
+            take_all(income_ref.at[it, half, others], income_send.at[it, half])
         for copy in besides:
             copy.wait_recv()
         moving = [moving_ref[it, p] for p in range(2)]
@@ -389,23 +488,21 @@
                 send(
                     low_ref.at[it + 1, half],
                     gather_ref.at[it + 1, coil, half],
-                    gather_send.at[it + 1],
+                    gather_send.at[it + 1, half],
                     gather_recv.at[it + 1, half],
                     {"coil": peer},
                 )
         if it < ITERS - 1:
             besides = greet(it + 1)
             pending.extend(besides)
+            for half in range(halves):
+                take_all(gather_ref.at[it + 1, others, half], gather_send.at[it + 1, half])
         momentum = following
 
     take_all(tallies_ref.at[others], tally_recv.at[0])
     misfit_ref[...] = jnp.sum(tallies_ref[...], axis=0)[:, :ITERS]
     for copy in pending:
         copy.wait_send()
-    for it in range(ITERS):
-        take_all(gather_ref.at[it, others], gather_send.at[it])
-        for half in range(halves):
-            take_all(income_ref.at[it, half, others], income_send.at[it, half])
     take_all(tallies_ref.at[others], tally_send.at[0])
 
 
@@ -430,14 +527,16 @@
         coil_maps,
         samples,
         *tables,
+        blocks_used,
     )
-    scalars = (1, 2)
+    scalars = (1, 2, 11)
     held = [
         (pltpu.SMEM if place in scalars else pltpu.VMEM)(operand.shape, operand.dtype)
         for place, operand in enumerate(operands)
     ]
     shard = (2, rows, size)
     halves = size // LANES
+    along = far_first(coils)[1]
     dma = pltpu.SemaphoreType.DMA
     doubled, misfit = pl.pallas_call(
         functools.partial(kernel, coils, frames),
@@ -445,7 +544,7 @@
             pltpu.VMEM((2 * rows * size // LANES, LANES), F32),
             pltpu.VMEM((1, ITERS), F32),
         ),
-        in_specs=[pl.BlockSpec(memory_space=pltpu.SMEM)] + [pl.BlockSpec(memory_space=pl.ANY)] * len(operands),
+        in_specs=[pl.BlockSpec(memory_space=pl.ANY)] * len(operands),
         out_specs=(vmem, vmem),
         scratch_shapes=held
         + [
@@ -463,7 +562,9 @@
             pltpu.VMEM((ITERS, 2) + shard, F32),
             pltpu.VMEM((1, LANES), F32),
             pltpu.VMEM((coils, 1, LANES), F32),
-            dma((ITERS,)),
+            dma((along,)),
+            dma((along,)),
+            dma((ITERS, halves)),
             dma((ITERS, halves)),
             dma((ITERS, halves)),
             dma((ITERS, halves)),
@@ -471,11 +572,13 @@
             dma((1,)),
             dma((ITERS, 2)),
             dma((ITERS, 2)),
+            pltpu.SemaphoreType.REGULAR((along,)),
+            dma((1,)),
         ],
         compiler_params=pltpu.CompilerParams(
             collective_id=0, has_side_effects=True, vmem_limit_bytes=56 * 1024 * 1024
         ),
-    )(blocks_used, *operands)
+    )(*operands)
     updated = (doubled * 0.5).reshape(rows, size // LANES, 2, LANES).transpose(0, 2, 1, 3)
     scale = 0.5 / (coils * blocks * spoke)
     return updated.reshape(image.shape), jnp.transpose(misfit * scale)

time: 55.8 us -> 59.3 us (1.063)
  the two profiles are of different devices: /device:TPU:16 before, /device:TPU:24 now
where the time goes in v5:
time: 59.3 us
  Pallas kernels  56.9 us (96%)
  between operations  1.29 us (2%)
  other arithmetic  1.12 us (2%)
    pallas_call x1, Pallas kernels, on_device(): pl.pallas_call(functools.partial(kernel, coils, frames), out_shape=(pltpu...  56.9 us

profile of v5, /device:TPU:24, one launch (start us, length us, event | category | flops | bytes accessed | tf_op | source)
XLA Modules:
  0.0 59.3 jit_solution(15431612557061783076)
XLA Ops:
  1.3 56.9 %shard_map.131 = (f32[32,128]{1,0:T(8,128)S(1)}, f32[1,2]{1,0:T(1,128)S(1)}) custom-call(f32[8,1,2,256]{3,2,1,0:T(2,128)} %refs_0_.1, s32[1,18]{1,0:T(1,128)} %refs_1_.1, s32[1,18]{1,0:T(1,128)} %refs_2_.1, s32[18,1,256]{2,1,0:T(1,128)} %bitcast.9, s32[18,1,256]{2,1,0:T(1,128)} %bitcast.10, bf16[1,18,4,256]{3,2,1,0:T(4,128)(2,1)} %refs_5_.1, ...), custom_call_target="tpu_custom_call" | custom-call | tf_op jit(solution)/shard_map/pallas_call | solution.py:541
  58.1 0.6 %broadcast_multiply_fusion = f32[32,128]{1,0:T(8,128)} fusion(f32[32,128]{1,0:T(8,128)S(1)} %get-tuple-element.4), kind=kLoop, calls=%fused_computation | loop fusion | flops 4096 | bytes 32768 | tf_op jit(solution)/shard_map/mul | solution.py:582
  58.7 0.5 multiply_bitcast_fusion

commit v6 on v2

--- a/solution.py
+++ b/solution.py
@@ -13,6 +13,7 @@
 ITERS = 2
 GROUP = 9
 EARLY = 6
+LAG = 3
 LANES = 128
 TILE = 128
 PACK = 16
@@ -44,7 +45,7 @@
         return 2 * min(dx, across - dx) + min(dz, along - dz)
 
     shifts = [(dx, dz) for dx in range(across) for dz in range(along) if dx or dz]
-    return across, along, sorted(shifts, key=hops, reverse=True)
+    return across, along, hops, sorted(shifts, key=hops, reverse=True)
 
 
 def dot(left, right):
@@ -106,11 +107,11 @@
     image_ref, misfit_ref = refs[11:13]
     held = refs[13:24]
     input_sem = refs[24]
-    loads = []
-    for place, (source, target) in enumerate(zip(inputs, held)):
-        copy = pltpu.make_async_copy(source, target, input_sem.at[place])
-        copy.start()
-        loads.append(copy)
+    loads = [
+        pltpu.make_async_copy(source, target, input_sem.at[place])
+        for place, (source, target) in enumerate(zip(inputs, held))
+    ]
+    loads[0].start()
     run(coils, frames, loads, used_ref, *held, image_ref, misfit_ref, *refs[25:])
 
 
@@ -167,7 +168,7 @@
     lanes = [slice(half * LANES, (half + 1) * LANES) for half in range(halves)]
     later = lax.rem(frame + 1, frames)
     earlier = lax.rem(frame + frames - 1, frames)
-    across, along, shifts = far_first(coils)
+    across, along, hops, shifts = far_first(coils)
     coil_x = coil // along
     coil_z = lax.rem(coil, along)
     peers = [lax.rem(coil_x + dx, across) * along + lax.rem(coil_z + dz, along) for dx, dz in shifts]
@@ -177,6 +178,8 @@
         pl.semaphore_signal(barrier, inc=1, device_id={"coil": peer}, device_id_type=MESH)
     for nearby in (later, earlier):
         pl.semaphore_signal(barrier, inc=1, device_id={"frame": nearby}, device_id_type=MESH)
+    for load in loads[1:]:
+        load.start()
 
     loads[0].wait()
     value = [start_ref[:, 0, p, :] for p in range(2)]
@@ -239,16 +242,16 @@
         ]
 
     for peer in peers:
-        send(low_ref.at[0], gather_ref.at[0, coil], gather_send.at[0], gather_recv.at[0, 0], {"coil": peer})
+        send(low_ref.at[0], gather_ref.at[0, coil], gather_send.at[0, 0], gather_recv.at[0, 0], {"coil": peer})
     besides = greet(0)
     pending = list(besides)
     lax.fori_loop(early, blocks, build, 0)
+    others = pl.ds(0, coils - 1)
     for place in range(7, 11):
         loads[place].wait()
     group = max(d for d in range(1, GROUP + 1) if blocks % d == 0)
     used = used_ref[0]
     momentum = 1.0
-    others = pl.ds(0, coils - 1)
 
     def first_half(pieces, cols):
         real, imag = pieces[:, :rows], pieces[:, rows:]
@@ -325,6 +328,24 @@
         spread = grid_ref[...].astype(BF16)
         back_half = dot(minus_ref[...], spread).astype(BF16)
         back_half = jnp.concatenate([back_half[:size], back_half[size:]], axis=1)
+
+        def give(half, turn):
+            send(
+                outgo_ref.at[it, peers[turn], half] if split else outgo_ref.at[it, peers[turn]],
+                income_ref.at[it, coil, half] if split else income_ref.at[it, coil],
+                income_send.at[it, half],
+                income_recv.at[it, half],
+                {"coil": peers[turn]},
+            )
+
+        split = it < ITERS - 1
+        if split:
+            order = sorted(
+                ((hops(shift) - LAG * half, half, turn) for half in range(halves) for turn, shift in enumerate(shifts)),
+                key=lambda entry: -entry[0],
+            )
+        else:
+            order = [(0, halves - 1, turn) for turn in range(coils - 1)]
         for half in range(halves):
             beyond = slice(size + half * LANES, size + (half + 1) * LANES)
             coil_back = dot(back_half, jnp.concatenate([plus_ref[:, lanes[half]], plus_ref[:, beyond]], axis=1))
@@ -334,20 +355,22 @@
             back_imag = coil_back[:, LANES:]
             real = (map_real * back_real + map_imag * back_imag).reshape(coils, rows, LANES)
             imag = (map_real * back_imag - map_imag * back_real).reshape(coils, rows, LANES)
-            outgo_ref[it, half] = jnp.concatenate([real, imag], axis=1).astype(BF16)
-            for peer in peers:
-                send(
-                    outgo_ref.at[it, half, peer],
-                    income_ref.at[it, half, coil],
-                    income_send.at[it, half],
-                    income_recv.at[it, half],
-                    {"coil": peer},
-                )
-            income_ref[it, half, coil] = outgo_ref[it, half, coil]
+            outgo_ref[it, :, half] = jnp.concatenate([real, imag], axis=1).astype(BF16)
+            while order and order[0][1] <= half:
+                _, which, turn = order.pop(0)
+                give(which, turn)
+        income_ref[it, coil] = outgo_ref[it, coil]
         if it == ITERS - 1:
             for peer in peers:
                 send(tally_ref, tallies_ref.at[coil], tally_send.at[0], tally_recv.at[0], {"coil": peer})
 
+        if it == 0:
+            take_all(gather_ref.at[0, others], gather_send.at[0, 0])
+        if split:
+            for half in range(halves):
+                take_all(income_ref.at[it, others, half], income_send.at[it, half])
+        else:
+            take_all(income_ref.at[it, others], income_send.at[it, halves - 1])
         for copy in besides:
             copy.wait_recv()
         moving = [moving_ref[it, p] for p in range(2)]
@@ -362,8 +385,11 @@
 
         for half in range(halves):
             part = lanes[half]
-            take_all(income_ref.at[it, half, others], income_recv.at[it, half])
-            sums = jnp.sum(income_ref[it, half].astype(F32), axis=0)
+            if split:
+                take_all(income_ref.at[it, others, half], income_recv.at[it, half])
+            elif half == 0:
+                take_all(income_ref.at[it, others], income_recv.at[it, halves - 1])
+            sums = jnp.sum(income_ref[it, :, half].astype(F32), axis=0)
             descent = [
                 moving[p][:, part] - step_size * (sums[p * rows : (p + 1) * rows] + tv_weight * variation[p][:, part])
                 for p in range(2)
@@ -389,23 +415,21 @@
                 send(
                     low_ref.at[it + 1, half],
                     gather_ref.at[it + 1, coil, half],
-                    gather_send.at[it + 1],
+                    gather_send.at[it + 1, half],
                     gather_recv.at[it + 1, half],
                     {"coil": peer},
                 )
         if it < ITERS - 1:
             besides = greet(it + 1)
             pending.extend(besides)
+            for half in range(halves):
+                take_all(gather_ref.at[it + 1, others, half], gather_send.at[it + 1, half])
         momentum = following
 
     take_all(tallies_ref.at[others], tally_recv.at[0])
     misfit_ref[...] = jnp.sum(tallies_ref[...], axis=0)[:, :ITERS]
     for copy in pending:
         copy.wait_send()
-    for it in range(ITERS):
-        take_all(gather_ref.at[it, others], gather_send.at[it])
-        for half in range(halves):
-            take_all(income_ref.at[it, half, others], income_send.at[it, half])
     take_all(tallies_ref.at[others], tally_send.at[0])
 
 
@@ -458,12 +482,12 @@
             pltpu.VMEM(shard, F32),
             pltpu.VMEM((ITERS, halves, 2 * rows, LANES), BF16),
             pltpu.VMEM((ITERS, coils, halves, 2 * rows, LANES), BF16),
-            pltpu.VMEM((ITERS, halves, coils, 2 * rows, LANES), BF16),
-            pltpu.VMEM((ITERS, halves, coils, 2 * rows, LANES), BF16),
+            pltpu.VMEM((ITERS, coils, halves, 2 * rows, LANES), BF16),
+            pltpu.VMEM((ITERS, coils, halves, 2 * rows, LANES), BF16),
             pltpu.VMEM((ITERS, 2) + shard, F32),
             pltpu.VMEM((1, LANES), F32),
             pltpu.VMEM((coils, 1, LANES), F32),
-            dma((ITERS,)),
+            dma((ITERS, halves)),
             dma((ITERS, halves)),
             dma((ITERS, halves)),
             dma((ITERS, halves)),

time: 55.8 us -> 56.8 us (1.018)
  the two profiles are of different devices: /device:TPU:16 before, /device:TPU:24 now
where the time goes in v6:
time: 56.8 us; the launch traced here: 56.6 us
  Pallas kernels  54.2 us (95%)
  between operations  1.29 us (2%)
  other arithmetic  1.12 us (2%)
    pallas_call x1, Pallas kernels, on_device(): pl.pallas_call(functools.partial(kernel, coils, frames), out_shape=(pltpu...  54.2 us

profile of v6, /device:TPU:24, one launch (start us, length us, event | category | flops | bytes accessed | tf_op | source)
XLA Modules:
  0.0 56.6 jit_solution(8262567091055084495)
XLA Ops:
  1.3 54.2 %shard_map.131 = (f32[32,128]{1,0:T(8,128)S(1)}, f32[1,2]{1,0:T(1,128)S(1)}) custom-call(s32[1]{0:T(128)S(6)} %copy.15.used_ref, f32[8,1,2,256]{3,2,1,0:T(2,128)} %refs_0_.1, s32[1,18]{1,0:T(1,128)} %refs_1_.1, s32[1,18]{1,0:T(1,128)} %refs_2_.1, s32[18,1,256]{2,1,0:T(1,128)} %bitcast.9, s32[18,1,256]{2,1,0:T(1,128)} %bitcast.10, ...), custom_call_target="tpu_custom_call" | custom-call | tf_op jit(solution)/shard_map/pallas_call | solution.py:466
  55.5 0.6 %broadcast_multiply_fusion = f32[32,128]{1,0:T(8,128)} fusion(f32[32,128]{1,0:T(8,128)S(1)} %get-tuple-element.4), kind=kLoop, calls=%fused_computation | loop fusion | flops 4096 | bytes 32768 | tf_op jit(solution)/shard_map/mul | solution.py:503
  56.1 0.5 multiply_bitcast_fusion
